TPU v7x, 32 devices: a whole 2x2x4 slice. The times are simulated.
32 devices in a mesh: dp: 4 (over x, core), ctx: 8 (over z, y).
Axes of the slice: x: 2, y: 2, z: 4, core: 2. Of those that a mesh axis runs over, the one named last changes fastest.
Arguments:
- tokens: bfloat16 [4, 4096, 2048], P('dp', 'ctx'), may hold values from -6 to 6
- in_weight: bfloat16 [2048, 5120], P(None, 'dp'), may hold values from -0.125 to 0.125
- step_weight: bfloat16 [2048, 64], replicated, may hold values from -0.125 to 0.125
- step_bias: float32 [64], replicated, may hold values from -3 to 0
- decay_rate: float32 [64], replicated, may hold values from 0.0001 to 0.5
- skip_gain: float32 [64], replicated, may hold values from 0.5 to 1.5
- filter_taps: float32 [4, 5120], replicated, may hold values from -3 to 3
- filter_bias: float32 [5120], replicated, may hold values from -3 to 3
- norm_gain: float32 [4096], replicated, may hold values from 0.5 to 1.5
Outputs:
- normed: bfloat16 [4, 4096, 4096], P('dp', 'ctx')
All inputs are finite; a program needn't handle non-finite values.
Results may differ from a plain program's by a relative error of at most 0.0061.
Values may be sent and summed in bfloat16 or wider, within the bound.
A program may use at most 192 MiB of HBM per device.

v0:
```python
import math

import jax
import jax.numpy as jnp
from jax import lax
from jax.sharding import PartitionSpec as P

HEADS = 64
HEAD_DIM = 64
STATE = 128
GROUPS = 4
BLOCK = 256
GROUP_HEADS = 16


def shifted(value, axis, steps):
    count = lax.axis_size(axis)
    initial, last = (max(0, -steps), min(count, count - steps))
    return lax.ppermute(value, axis, [(source, source + steps) for source in range(initial, last)])


def filter_rows(prefix, current, filter_taps, filter_bias):
    padded = jnp.concatenate([prefix, current], axis=0).astype(jnp.float32)
    length = current.shape[0]
    summed = filter_bias + filter_taps[0] * padded[0:length]
    for offset in range(1, filter_taps.shape[0]):
        summed = summed + filter_taps[offset] * padded[offset : offset + length]
    return summed


def ssd_group(values, input_map, output_map, step_size, decay_rate, skip_gain, block_len):
    length, head_count, head_width = values.shape
    block_count = length // block_len
    bundle = math.gcd(block_count, 8)
    bundle_count = block_count // bundle
    highest = lax.Precision.HIGHEST
    value_rows = values.reshape(block_count, block_len, head_count, head_width)
    input_rows = input_map.reshape(block_count, block_len, -1)
    output_rows = output_map.reshape(block_count, block_len, -1)
    step_rows = step_size.reshape(block_count, block_len, head_count)
    decay_sum = jnp.cumsum(-step_rows * decay_rate, axis=1)
    causal = (jnp.arange(block_len)[:, None] >= jnp.arange(block_len)[None, :])[None, :, :, None]

    def local_block(pieces):
        value_block, input_block, output_block, step_block, decay_block = pieces
        scores = jnp.einsum(
            "ktn,kun->ktu", output_block, input_block, preferred_element_type=jnp.float32
        )
        decay_gap = jnp.where(causal, decay_block[:, :, None, :] - decay_block[:, None, :, :], 0.0)
        weights = (
            jnp.where(causal, jnp.exp(decay_gap), 0.0)
            * scores[..., None]
            * step_block[:, None, :, :]
        ).astype(jnp.bfloat16)
        within = jnp.einsum(
            "ktuh,kuhp->kthp", weights, value_block, preferred_element_type=jnp.float32
        )
        to_end = jnp.exp(decay_block[:, -1:, :] - decay_block) * step_block
        scaled = (to_end[..., None] * value_block.astype(jnp.float32)).astype(jnp.bfloat16)
        states = jnp.einsum(
            "kuhp,kun->khpn", scaled, input_block, preferred_element_type=jnp.float32
        )
        return (within, states)

    def blocked(array):
        return array.reshape((bundle_count, bundle) + array.shape[1:])

    within, states = lax.map(
        local_block,
        (
            blocked(value_rows),
            blocked(input_rows),
            blocked(output_rows),
            blocked(step_rows),
            blocked(decay_sum),
        ),
    )
    within = within.reshape(block_count, block_len, head_count, head_width)
    states = states.reshape((block_count,) + states.shape[2:])
    totals = decay_sum[:, -1, :]
    running = jnp.cumsum(totals, axis=0)
    starts = running - totals
    before = (jnp.arange(block_count)[:, None] > jnp.arange(block_count)[None, :])[:, :, None]
    mixing = jnp.where(
        before, jnp.exp(jnp.where(before, starts[:, None, :] - running[None, :, :], 0.0)), 0.0
    )
    entering = jnp.einsum("kjh,jhpn->khpn", mixing, states, precision=highest)
    carried = (
        jnp.einsum("khpn,ktn->kthp", entering, output_rows.astype(jnp.float32), precision=highest)
        * jnp.exp(decay_sum)[..., None]
    )
    output = within + carried + skip_gain[:, None] * value_rows.astype(jnp.float32)
    return output.reshape(length, head_count, head_width)


def group_norm(values, norm_gain):
    length = values.shape[0]
    grouped = values.astype(jnp.float32).reshape(length, GROUPS, -1)
    mean_square = jnp.mean(jnp.square(grouped), axis=-1, keepdims=True)
    return (grouped * lax.rsqrt(mean_square + 1e-05)).reshape(length, -1) * norm_gain


def sequence_filter(projected, filter_taps, filter_bias):
    reach_rows = filter_taps.shape[0] - 1
    length = projected.shape[0]
    rim_rows = shifted(projected[length - reach_rows :], "ctx", 1)
    return jax.nn.silu(filter_rows(rim_rows, projected, filter_taps, filter_bias)).astype(
        jnp.bfloat16
    )


def head_layout(source, step_raw, step_bias, decay_rate, skip_gain):
    context_size = lax.axis_size("ctx")
    device = lax.axis_index("ctx")
    length = source.shape[0]
    inner_width = HEADS * HEAD_DIM
    local_heads = HEADS // context_size
    local_width = local_heads * HEAD_DIM
    group_share = max(1, GROUP_HEADS // local_heads)
    local_groups = max(1, local_heads // GROUP_HEADS)
    value_parts = source[:, :inner_width].reshape(length, context_size, local_width)
    map_parts = source[:, inner_width:].reshape(length, 2, GROUPS, STATE)
    map_parts = jnp.repeat(map_parts, group_share, axis=2)
    step_parts = step_raw.reshape(length, context_size, local_heads)
    moved_values, moved_input, moved_output, moved_steps = (
        lax.all_to_all(value_parts, "ctx", split_axis=1, concat_axis=0, tiled=True),
        lax.all_to_all(map_parts[:, 0], "ctx", split_axis=1, concat_axis=0, tiled=True),
        lax.all_to_all(map_parts[:, 1], "ctx", split_axis=1, concat_axis=0, tiled=True),
        lax.all_to_all(step_parts, "ctx", split_axis=1, concat_axis=0, tiled=True),
    )
    full_length = moved_values.shape[0]
    head_values = moved_values.reshape(full_length, local_width)
    input_maps = moved_input.reshape(full_length, local_groups * STATE)
    output_maps = moved_output.reshape(full_length, local_groups * STATE)
    bias_slice = lax.dynamic_slice_in_dim(step_bias, device * local_heads, local_heads, 0)
    rate_slice = lax.dynamic_slice_in_dim(decay_rate, device * local_heads, local_heads, 0)
    skip_slice = lax.dynamic_slice_in_dim(skip_gain, device * local_heads, local_heads, 0)
    step_size = jax.nn.softplus(
        moved_steps.reshape(full_length, local_heads).astype(jnp.float32) + bias_slice
    )
    inputs = head_values.reshape(full_length, local_heads, HEAD_DIM)
    pieces = ssd_group(inputs, input_maps, output_maps, step_size, rate_slice, skip_slice, BLOCK)
    mixed_rows = pieces.reshape(full_length, local_width).astype(jnp.bfloat16)
    return lax.all_to_all(mixed_rows, "ctx", split_axis=0, concat_axis=1, tiled=True)


def per_device(
    tokens,
    in_weight,
    step_weight,
    step_bias,
    decay_rate,
    skip_gain,
    filter_taps,
    filter_bias,
    norm_gain,
):
    token_rows = tokens[0]
    projected = jnp.dot(
        token_rows,
        lax.all_gather(in_weight, "dp", axis=1, tiled=True),
        preferred_element_type=jnp.float32,
    ).astype(jnp.bfloat16)
    step_raw = jnp.dot(token_rows, step_weight, preferred_element_type=jnp.float32).astype(
        jnp.bfloat16
    )
    active = sequence_filter(projected, filter_taps, filter_bias)
    mixed_rows = head_layout(active, step_raw, step_bias, decay_rate, skip_gain)
    return group_norm(mixed_rows, norm_gain).astype(jnp.bfloat16)[None]


def solution(mesh):
    in_specs = (P("dp", "ctx", None), P(None, "dp"), P(), P(), P(), P(), P(), P(), P())
    out_specs = P("dp", "ctx", None)
    return jax.shard_map(
        per_device, mesh=mesh, in_specs=in_specs, out_specs=out_specs, check_vma=False
    )
```

profile of v0, /device:TPU:0, one launch (start us, length us, event | category | flops | bytes accessed | tf_op | source)
XLA Modules:
  0.0 554.3 jit_solution(2078704967498910302)
XLA Ops:
  7.3 0.9 copy-done
  8.1 2.3 fusion.45
  10.5 7.3 %all-to-all-start.1 = ((bf16[512,8,8]{0,2,1:T(8,128)(2,1)}), bf16[512,8,8]{0,2,1:T(8,128)(2,1)S(1)}, u32[]{:S(2)}, u32[]{:S(2)}) async-start(bf16[512,8,8]{0,2,1:T(8,128)(2,1)} %fusion.45), calls=%async_computation.1 | async-start | bytes 131072 | tf_op jit(solution)/shard_map/all_to_all | solution.py:129
  17.8 125.4 %all-gather.2.cloned.1.call-done = bf16[2048,5120]{1,0:T(8,128)(2,1)} async-done(((bf16[2048,1280]{1,0:T(8,128)(2,1)}), bf16[2048,5120]{1,0:T(8,128)(2,1)}) %all-gather.2.cloned.1.call-update) | async-done | bytes 20971536 | tf_op jit(solution)/shard_map/all_gather | solution.py:161
  143.2 15.1 %convolution_convert_fusion = bf16[512,5120]{1,0:T(8,128)(2,1)S(1)} fusion(bf16[2048,5120]{1,0:T(8,128)(2,1)} %all-gather.2.cloned.1.call-done, bf16[1,512,2048]{2,1,0:T(8,128)(2,1)S(1)} %copy-done), kind=kOutput, calls=%fused_computation.49 | convolution fusion | flops 10740039680 | bytes 28311552 | tf_op jit(solution)/shard_map/dot_general | solution.py:159
  158.4 3.4 collective-permute-start
  161.9 1.6 collective-permute-done
  163.5 1.5 maximum_convert_fusion
  165.0 6.7 %multiply_convert_fusion.8 = bf16[512,5120]{1,0:T(8,128)(2,1)S(1)} fusion(f32[515,5120]{1,0:T(8,128)S(1)} %maximum_convert_fusion, f32[5120]{0:T(1024)S(1)} %bitcast.192, f32[5120]{0:T(1024)S(1)} %bitcast.193, f32[5120]{0:T(1024)S(1)} %bitcast.191, f32[5120]{0:T(1024)S(1)} %bitcast.190, f32[5120]{0:T(1024)S(1)} %copy-done.7), kind=kLoop, calls=%fused_computation.40 | loop fusion | flops 34078720 | bytes 47288320 | tf_op jit(solution)/shard_map/convert_element_type | solution.py:107
  171.8 2.3 copy-done.5
  174.1 0.8 reshape.188
  175.5 1.6 slice_bitcast_fusion.1
  177.0 6.4 %all-to-all-start.2 = ((bf16[512,8,128]{2,0,1:T(8,128)(2,1)}), bf16[512,8,128]{2,0,1:T(8,128)(2,1)}, u32[]{:S(2)}, u32[]{:S(2)}) async-start(bf16[512,8,128]{2,0,1:T(8,128)(2,1)} %get-tuple-element.173), calls=%async_computation.2 | async-start | bytes 2097152 | tf_op jit(solution)/shard_map/all_to_all | solution.py:128
  183.4 4.7 slice.75
  188.1 6.5 %copy.167 = bf16[512,4096]{0,1:T(8,128)(2,1)} copy(bf16[512,4096]{1,0:T(8,128)(2,1)} %slice.75) | data formatting | bytes 8388608 | tf_op jit(solution)/shard_map/reshape | solution.py:121
  194.6 14.2 %all-to-all-done.2 = bf16[512,8,128]{2,0,1:T(8,128)(2,1)} async-done(((bf16[512,8,128]{2,0,1:T(8,128)(2,1)}), bf16[512,8,128]{2,0,1:T(8,128)(2,1)}, u32[]{:S(2)}, u32[]{:S(2)}) %all-to-all-start.2) | async-done | bytes 1048608 | tf_op jit(solution)/shard_map/all_to_all | solution.py:128
  208.8 4.6 all-to-all-start
  214.2 91.4 %all-to-all-done = bf16[512,8,512]{0,2,1:T(8,128)(2,1)} async-done(((bf16[512,8,512]{0,2,1:T(8,128)(2,1)}), bf16[512,8,512]{0,2,1:T(8,128)(2,1)}, u32[]{:S(2)}, u32[]{:S(2)}) %all-to-all-start) | async-done | bytes 4194336 | tf_op jit(solution)/shard_map/all_to_all | solution.py:126
  305.6 4.4 all-to-all-start.3
  310.2 9.0 %reduce-window.6 = f32[16,8,2,128]{3,1,2,0:T(8,128)S(1)} reduce-window(f32[16,8,2,128]{3,1,2,0:T(8,128)S(1)} %fusion.50, f32[]{:T(128)} %constant.30.clone.1), window={size=1x1x1x128 pad=0_0x0_0x0_0x127_0}, to_apply=%region_0.1 | reduce-window | flops 4161536 | bytes 262148 | tf_op jit(solution)/shard_map/reduce-window
  321.2 6.5 %copy.143 = bf16[8,512,1,512]{1,0,3,2:T(8,128)(2,1)} copy(bf16[8,512,1,512]{1,3,0,2:T(8,128)(2,1)} %bitcast.7) | data formatting | bytes 8388608 | tf_op jit(solution)/shard_map/all_to_all | solution.py:126
  327.6 7.1 %reshape_reshape_reshape_reshape.3 = bf16[2,8,256,8,64]{2,1,0,4,3:T(8,128)(2,1)} reshape(bf16[8,512,1,512]{1,0,3,2:T(8,128)(2,1)} %copy.143) | data formatting | bytes 8388608 | tf_op jit(solution)/shard_map/reshape;reshape;reshape;reshape | solution.py:66
  334.8 0.9 all-to-all-done.3
  335.6 34.5 %while.14 = (s32[]{:T(128)}, f32[2,8,256,8,64]{2,4,3,1,0:T(8,128)}, f32[2,8,8,64,128]{4,3,2,1,0:T(8,128)}, bf16[2,8,256,8,64]{2,1,0,4,3:T(8,128)(2,1)}, f32[2,8,...) while((s32[]{:T(128)}, f32[2,8,256,8,64]{2,4,3,1,0:T(8,128)}, ...), condition=%wide.region_3.4_spmd.clone.clone, body=%wide.region_2.3_spmd.clone.clone.sunk | while | flops 967933952 | bytes 30084480 | solution.py:68
  335.6 1.6 fusion.77
  337.3 1.7 constant_dynamic-slice_fusion.6
  339.1 1.3 copy-done.2
  340.4 7.4 %bitcast_dynamic-update-slice_fusion.4 = f32[2,8,256,8,64]{2,4,3,1,0:T(8,128)} fusion(f32[2,8,256,8,64]{2,4,3,1,0:T(8,128)} %get-tuple-element.241, s32[]{:T(128)} %get-tuple-element.240, f32[8,256,8]{1,2,0:T(8,128)S(1)} %bitcast.182, f32[8,256,256]{2,1,0:T(8,128)S(1)} %fusion.77, f32[8,256,8]{1,2,0:T(8,128)S(1)} %bitcast.183, ...), kind=kOutput, calls=%fused_computation.9.clone.1 | convolution fusion | flops 562036736 | bytes 8651264 | tf_op jit(solution)/shard_map/while/body/eval_jaxpr/ktuh,kuhp->kthp/dot_general | solution.py:55
  349.1 3.7 bitcast_dynamic-update-slice_fusion.5
  352.9 1.6 fusion.77
  354.5 1.7 constant_dynamic-slice_fusion.6
  356.3 1.3 copy-done.2
  357.6 7.4 %bitcast_dynamic-update-slice_fusion.4 = f32[2,8,256,8,64]{2,4,3,1,0:T(8,128)} fusion(f32[2,8,256,8,64]{2,4,3,1,0:T(8,128)} %get-tuple-element.241, s32[]{:T(128)} %get-tuple-element.240, f32[8,256,8]{1,2,0:T(8,128)S(1)} %bitcast.182, f32[8,256,256]{2,1,0:T(8,128)S(1)} %fusion.77, f32[8,256,8]{1,2,0:T(8,128)S(1)} %bitcast.183, ...), kind=kOutput, calls=%fused_computation.9.clone.1 | convolution fusion | flops 562036736 | bytes 8651264 | tf_op jit(solution)/shard_map/while/body/eval_jaxpr/ktuh,kuhp->kthp/dot_general | solution.py:55
  366.4 3.7 bitcast_dynamic-update-slice_fusion.5
  370.1 3.4 bitcast_convert_fusion.1
  373.5 8.1 %copy.158 = f32[8,512,1,512]{1,0,3,2:T(8,128)} copy(f32[8,512,1,512]{1,3,0,2:T(8,128)S(1)} %bitcast_convert_fusion.1) | data formatting | bytes 16777216 | tf_op jit(solution)/shard_map/convert_element_type | solution.py:92
  381.6 9.5 %reshape.194 = f32[16,256,8,64]{1,0,3,2:T(8,128)} reshape(f32[8,512,1,512]{1,0,3,2:T(8,128)} %copy.158) | data formatting | bytes 16777216 | tf_op jit(solution)/shard_map/convert_element_type | solution.py:92
  391.1 10.2 %fusion.36 = f32[16,8,64,128]{3,0,2,1:T(8,128)} fusion(f32[16,8,64,128]{3,2,1,0:T(8,128)} %bitcast.186, f32[16,8]{0,1:T(8,128)S(1)} %copy.153, f32[16,8]{0,1:T(8,128)S(1)} %fusion.62, pred[16,16]{1,0:T(8,128)(4,1)S(1)} %iota_compare_fusion.1), kind=kOutput, calls=%fused_computation.55 | convolution fusion | flops 201332736 | bytes 8389888 | tf_op jit(solution)/shard_map/kjh,jhpn->khpn/dot_general | solution.py:87
  401.3 15.9 %fusion.29 = bf16[16,256,8,64]{1,3,2,0:T(8,128)(2,1)} fusion(f32[2,8,256,8,64]{2,4,3,1,0:T(8,128)} %get-tuple-element.56, f32[16,256,8,64]{1,0,3,2:T(8,128)S(1)} %copy-done.4, f32[8]{0:T(128)S(1)} %copy-done.9, f32[16,256,8]{1,2,0:T(8,128)S(1)} %copy.157, bf16[16,256,128,1]{2,1,3,0:T(8,128)(2,1)} %bitcast.34, f32[16,8,64,128]{3,0,2,1:T(8,128)} %fusion.36), kind=kOutput, calls=%fused_computation.46 | convolution fusion | flops 3231711232 | bytes 26345504 | tf_op jit(solution)/shard_map/khpn,ktn->kthp/dot_general | solution.py:89
  417.2 6.7 %copy.160 = bf16[16,256,8,64]{1,0,3,2:T(8,128)(2,1)} copy(bf16[16,256,8,64]{1,3,2,0:T(8,128)(2,1)} %fusion.29) | data formatting | bytes 8388608 | tf_op jit(solution)/shard_map/convert_element_type | solution.py:143
  423.9 7.1 %convert_element_type.101 = bf16[8,512,512]{1,0,2:T(8,128)(2,1)} reshape(bf16[16,256,8,64]{1,0,3,2:T(8,128)(2,1)} %copy.160) | data formatting | bytes 8388608 | tf_op jit(solution)/shard_map/convert_element_type | solution.py:143
  431.0 3.6 copy.161
  434.6 97.4 %all_to_all.64 = bf16[8,512,512]{1,2,0:T(8,128)(2,1)S(1)} all-to-all(bf16[8,512,512]{1,2,0:T(8,128)(2,1)S(1)} %copy.161), channel_id=1, replica_groups=mesh['dp'=4,'ctx'=8] {'ctx'}, dimensions={0} | all-to-all | bytes 8388608 | tf_op jit(solution)/shard_map/all_to_all | solution.py:144
  532.0 2.0 copy-done.3
  534.0 0.8 multiply_reduce_fusion
  534.9 3.3 convert_element_type.116
  538.3 2.4 fusion.27
  540.7 6.3 %copy.163 = bf16[1,512,4096]{2,1,0:T(8,128)(2,1)} copy(bf16[1,512,4096]{1,2,0:T(8,128)(2,1)} %fusion.27) | data formatting | bytes 8388608 | tf_op jit(solution)/shard_map/convert_element_type | solution.py:169
  (72 shorter events, 7.0 us)
Async XLA Ops:
  6.5 1.6 copy-start
  6.5 136.7 %all-gather.2.cloned.1.call-start = ((), (), s32[]{:S(2)}) async-start(), calls=%async_computation.5 | async-start | bytes 26214400 | tf_op jit(solution)/shard_map/all_gather | solution.py:161
  10.5 166.6 %all-to-all-start.1 = ((bf16[512,8,8]{0,2,1:T(8,128)(2,1)}), bf16[512,8,8]{0,2,1:T(8,128)(2,1)S(1)}, u32[]{:S(2)}, u32[]{:S(2)}) async-start(bf16[512,8,8]{0,2,1:T(8,128)(2,1)} %fusion.45), calls=%async_computation.1 | async-start | bytes 131072 | tf_op jit(solution)/shard_map/all_to_all | solution.py:129
  17.8 144.0 %copy-start.6 = (f32[4,5120]{1,0:T(4,128)S(1)}, f32[4,5120]{1,0:T(4,128)}, u32[]{:S(2)}) copy-start(f32[4,5120]{1,0:T(4,128)} %param.17) | copy-start | bytes 245764
  158.4 6.6 %copy-start.7 = (f32[5120]{0:T(1024)S(1)}, f32[5120]{0:T(1024)}, u32[]{:S(2)}) copy-start(f32[5120]{0:T(1024)} %param.18) | copy-start | bytes 61444
  158.4 5.0 collective-permute-start
  171.8 2.3 copy-start.5
  177.0 31.7 %all-to-all-start.2 = ((bf16[512,8,128]{2,0,1:T(8,128)(2,1)}), bf16[512,8,128]{2,0,1:T(8,128)(2,1)}, u32[]{:S(2)}, u32[]{:S(2)}) async-start(bf16[512,8,128]{2,0,1:T(8,128)(2,1)} %get-tuple-element.173), calls=%async_computation.2 | async-start | bytes 2097152 | tf_op jit(solution)/shard_map/all_to_all | solution.py:128
  188.1 25.3 %copy-start.10 = (f32[64]{0:T(128)S(1)}, f32[64]{0:T(128)}, u32[]{:S(2)}) copy-start(f32[64]{0:T(128)} %param.14) | copy-start | bytes 772
  188.1 25.4 %copy-start.11 = (f32[64]{0:T(128)S(1)}, f32[64]{0:T(128)}, u32[]{:S(2)}) copy-start(f32[64]{0:T(128)} %param.15) | copy-start | bytes 772
  188.1 25.4 %copy-start.12 = (f32[64]{0:T(128)S(1)}, f32[64]{0:T(128)}, u32[]{:S(2)}) copy-start(f32[64]{0:T(128)} %param.16) | copy-start | bytes 772
  208.8 96.8 %all-to-all-start = ((bf16[512,8,512]{0,2,1:T(8,128)(2,1)}), bf16[512,8,512]{0,2,1:T(8,128)(2,1)}, u32[]{:S(2)}, u32[]{:S(2)}) async-start(bf16[512,8,512]{0,2,1:T(8,128)(2,1)} %bitcast.180), calls=%async_computation | async-start | bytes 8388608 | tf_op jit(solution)/shard_map/all_to_all | solution.py:126
  305.6 30.0 %all-to-all-start.3 = ((bf16[512,8,128]{2,0,1:T(8,128)(2,1)}), bf16[512,8,128]{2,0,1:T(8,128)(2,1)}, u32[]{:S(2)}, u32[]{:S(2)}) async-start(bf16[512,8,128]{2,0,1:T(8,128)(2,1)} %get-tuple-element.172), calls=%async_computation.3 | async-start | bytes 2097152 | tf_op jit(solution)/shard_map/all_to_all | solution.py:127
  339.0 1.3 copy-start.2
  356.2 1.3 copy-start.2
  391.1 10.3 %copy-start.4 = (f32[16,256,8,64]{1,0,3,2:T(8,128)S(1)}, f32[16,256,8,64]{1,0,3,2:T(8,128)}, u32[]{:S(2)}) copy-start(f32[16,256,8,64]{1,0,3,2:T(8,128)} %reshape.194) | copy-start | bytes 25165828
  391.1 10.3 %copy-start.9 = (f32[8]{0:T(128)S(1)}, f32[8]{0:T(128)}, u32[]{:S(2)}) copy-start(f32[8]{0:T(128)} %dynamic_slice.29) | copy-start | bytes 100
  532.0 2.0 copy-start.3
  534.0 4.3 copy-start.8
  538.3 8.8 %copy-start.1 = (bf16[1,512,2048]{2,1,0:T(8,128)(2,1)S(1)}, bf16[1,512,2048]{2,1,0:T(8,128)(2,1)}, u32[]{:S(2)}) copy-start(bf16[1,512,2048]{2,1,0:T(8,128)(2,1)} %param.11) | copy-start | bytes 6291460
Sparse Core Ops, SparseCore 0:
  8.9 134.2 all-gather.1
where the time goes:
time: 563 us; the launch traced here: 554 us
  waiting for transfers between devices  234 us (42%)
  blocking collectives  97.4 us (17%)
  local copies, waits for them, and re-layouts  85 us (15%)
  matrix products  69.2 us (12%)
  other arithmetic  28.3 us (5%)
  starting transfers between devices  26.1 us (5%)
  between operations  14.2 us (3%)
    all_gather x1, waiting for transfers between devices, per_device(): lax.all_gather(in_weight, 'dp', axis=1, tiled=True)  125 us
    all_to_all x1, blocking collectives, head_layout(): lax.all_to_all(mixed_rows, 'ctx', split_axis=0, concat_axis=1, tiled=True)  97.4 us
    all_to_all x1, waiting for transfers between devices, head_layout(): lax.all_to_all(value_parts, 'ctx', split_axis=1, concat_axis=0, tiled=True)  91.4 us
    convert_element_type x2, local copies, waits for them, and re-layouts, ssd_group(): value_rows.astype(jnp.float32)  17.6 us
    convert_element_type x3, local copies, waits for them, and re-layouts, head_layout(): mixed_rows = pieces.reshape(full_length, local_width).astype(jnp.bfloat16)  17.4 us
    dot_general x1, matrix products, ssd_group(): jnp.einsum('khpn,ktn->kthp', entering, output_rows.astype(jnp.float32), p...  15.9 us
    dot_general x1, matrix products, per_device(): jnp.dot(token_rows, lax.all_gather(in_weight, 'dp', axis=1, tiled=True),...  15.1 us
    dot_general x2, matrix products, local_block(): jnp.einsum('ktuh,kuhp->kthp', weights, value_block, preferred_element_typ...  14.9 us
  transfers between devices with their start and end apart: 6, of which 5 were waited for; matrix products, arithmetic and copies ran while one was open for 12% of the time, Pallas kernels for 0%

commit v1 on v0

v1 whole, which is shorter than its diff:
```python
import functools
import math

import jax
import jax.numpy as jnp
from jax import lax
from jax.experimental import pallas as pl
from jax.experimental.pallas import tpu as pltpu
from jax.sharding import PartitionSpec as P

HEADS = 64
HEAD_DIM = 64
STATE = 128
GROUPS = 4
BLOCK = 256
GROUP_HEADS = HEADS // GROUPS
GROUP_WIDTH = GROUP_HEADS * HEAD_DIM
INNER = HEADS * HEAD_DIM
RIM = 16
LOG2E = math.log2(math.e)
VMEM_LIMIT = 60 * 2**20


def project_kernel(rows_ref, weight_ref, taps_ref, bias_ref, active_ref):
    length = active_ref.shape[0]
    projected = jnp.dot(rows_ref[...], weight_ref[0], preferred_element_type=jnp.float32)
    projected = projected.astype(jnp.bfloat16).astype(jnp.float32)
    taps = taps_ref[...]
    count = taps.shape[0]
    summed = bias_ref[...] + taps[count - 1 : count] * projected[RIM:]
    for k in range(count - 1):
        first = RIM - (count - 1) + k
        summed = summed + taps[k : k + 1] * projected[first : first + length]
    active_ref[...] = (summed / (1.0 + jnp.exp(-summed))).astype(jnp.bfloat16)


def project(rows, weight, taps, bias, tile):
    length = rows.shape[0] - RIM
    shards, depth, width = weight.shape
    tiles = width // tile
    column = lambda s, j: (0, s * tiles + j)
    return pl.pallas_call(
        project_kernel,
        grid=(shards, tiles),
        in_specs=[
            pl.BlockSpec(rows.shape, lambda s, j: (0, 0)),
            pl.BlockSpec((1, depth, tile), lambda s, j: (s, 0, j)),
            pl.BlockSpec((taps.shape[0], tile), column),
            pl.BlockSpec((1, tile), column),
        ],
        out_specs=pl.BlockSpec((length, tile), column),
        out_shape=jax.ShapeDtypeStruct((length, shards * width), jnp.bfloat16),
        compiler_params=pltpu.CompilerParams(vmem_limit_bytes=VMEM_LIMIT),
        name="project",
    )(rows, weight, taps, bias)


def pair_columns(columns, pair, low_half):
    first = 2 * pair
    return jnp.where(low_half, columns[:, first : first + 1], columns[:, first + 1 : first + 2])


def block_state(values, input_map, ending, gap_columns, low_half):
    pieces = []
    for pair in range(GROUP_HEADS // 2):
        lanes = slice(pair * 128, (pair + 1) * 128)
        weight = jnp.exp2(ending[:, lanes] - pair_columns(gap_columns, pair, low_half))
        pieces.append((weight * values[:, lanes].astype(jnp.float32)).astype(jnp.bfloat16))
    scaled = jnp.concatenate(pieces, axis=1)
    return lax.dot_general(
        input_map, scaled, (((0,), (0,)), ((), ())), preferred_element_type=jnp.float32
    )


def low_mask(rows):
    return lax.broadcasted_iota(jnp.int32, (rows, 128), 1) < HEAD_DIM


def states_kernel(values_ref, input_ref, gap_ref, ending_ref, state_ref):
    blocks = values_ref.shape[0] // BLOCK
    low_half = low_mask(BLOCK)
    total = None
    for k in range(blocks):
        rows = pl.ds(k * BLOCK, BLOCK)
        ending = ending_ref[k]
        state = block_state(values_ref[rows, :], input_ref[rows, :], ending, gap_ref[0, rows, :], low_half)
        total = state if total is None else total * jnp.exp2(ending) + state
    chunks, _, width = state_ref.shape
    for chunk in range(chunks):
        state_ref[chunk] = total[:, chunk * width : (chunk + 1) * width].astype(jnp.bfloat16)


def device_states(active, gap, ending, parts):
    length = active.shape[0]
    chunks = parts // GROUPS
    blocks = length // BLOCK
    width = INNER // parts
    return pl.pallas_call(
        states_kernel,
        grid=(GROUPS,),
        in_specs=[
            pl.BlockSpec((length, GROUP_WIDTH), lambda g: (0, g)),
            pl.BlockSpec((length, STATE), lambda g: (0, INNER // STATE + g)),
            pl.BlockSpec((1, length, GROUP_HEADS), lambda g: (g, 0, 0)),
            pl.BlockSpec((blocks, 1, GROUP_WIDTH), lambda g: (0, 0, g)),
        ],
        out_specs=pl.BlockSpec((chunks, STATE, width), lambda g: (g, 0, 0)),
        out_shape=jax.ShapeDtypeStruct((parts, STATE, width), jnp.bfloat16),
        compiler_params=pltpu.CompilerParams(vmem_limit_bytes=VMEM_LIMIT),
        name="states",
    )(active, active, gap, ending)


def mix_kernel(
    values_ref,
    input_ref,
    output_ref,
    decay_ref,
    gap_ref,
    gap_row_ref,
    ending_ref,
    entering_ref,
    skip_ref,
    gain_ref,
    normed_ref,
    entering_scratch,
    mixed_scratch,
):
    blocks = values_ref.shape[0] // BLOCK
    half = BLOCK // 2
    low_half = low_mask(BLOCK)
    causal = lax.broadcasted_iota(jnp.int32, (half, half), 0) >= lax.broadcasted_iota(
        jnp.int32, (half, half), 1
    )
    chunks, _, width = entering_ref.shape
    for chunk in range(chunks):
        entering_scratch[:, chunk * width : (chunk + 1) * width] = entering_ref[chunk].astype(jnp.float32)
    for k in range(blocks):
        rows = pl.ds(k * BLOCK, BLOCK)
        input_map = input_ref[rows, :]
        output_map = output_ref[rows, :]
        scores = lax.dot_general(
            output_map, input_map, (((1,), (1,)), ((), ())), preferred_element_type=jnp.float32
        )
        decay = decay_ref[0, rows, :]
        gap_rows = gap_row_ref[0, :, rows]
        carried = jnp.dot(
            output_map, entering_scratch[...].astype(jnp.bfloat16), preferred_element_type=jnp.float32
        )
        squares = jnp.zeros((BLOCK, 128), jnp.float32)
        for pair in range(GROUP_HEADS // 2):
            lanes = slice(pair * 128, (pair + 1) * 128)
            values = values_ref[rows, lanes]
            within = []
            for head in (2 * pair, 2 * pair + 1):
                column = decay[:, head : head + 1]
                row = gap_rows[head : head + 1, :]
                top = jnp.where(causal, column[:half] - row[:, :half], -jnp.inf)
                top = (jnp.exp2(top) * scores[:half, :half]).astype(jnp.bfloat16)
                left = jnp.exp2(column[half:] - row[:, :half]) * scores[half:, :half]
                right = jnp.where(causal, column[half:] - row[:, half:], -jnp.inf)
                right = jnp.exp2(right) * scores[half:, half:]
                bottom = jnp.concatenate([left, right], axis=1).astype(jnp.bfloat16)
                within.append(
                    jnp.concatenate(
                        [
                            jnp.dot(top, values[:half], preferred_element_type=jnp.float32),
                            jnp.dot(bottom, values, preferred_element_type=jnp.float32),
                        ],
                        axis=0,
                    )
                )
            inside = jnp.where(low_half, within[0], within[1])
            growth = jnp.exp2(pair_columns(decay, pair, low_half))
            mixed = (
                inside
                + growth * carried[:, lanes]
                + skip_ref[:, lanes] * values.astype(jnp.float32)
            ).astype(jnp.bfloat16)
            mixed_scratch[:, lanes] = mixed
            wide = mixed.astype(jnp.float32)
            squares = squares + wide * wide
        mean = jnp.sum(squares, axis=1, keepdims=True) * (1.0 / GROUP_WIDTH)
        scale = lax.rsqrt(mean + 1e-05)
        normed_ref[rows, :] = (
            mixed_scratch[...].astype(jnp.float32) * scale * gain_ref[...]
        ).astype(jnp.bfloat16)
        if k < blocks - 1:
            ending = ending_ref[k]
            state = block_state(values_ref[rows, :], input_map, ending, gap_ref[0, rows, :], low_half)
            entering_scratch[...] = entering_scratch[...] * jnp.exp2(ending) + state


def mix(active, decay, gap, gap_rows, ending, entering, skip, gain):
    length = active.shape[0]
    blocks = length // BLOCK
    parts, _, width = entering.shape
    chunks = parts // GROUPS
    group_column = lambda g: (0, g)
    return pl.pallas_call(
        mix_kernel,
        grid=(GROUPS,),
        in_specs=[
            pl.BlockSpec((length, GROUP_WIDTH), group_column),
            pl.BlockSpec((length, STATE), lambda g: (0, INNER // STATE + g)),
            pl.BlockSpec((length, STATE), lambda g: (0, INNER // STATE + GROUPS + g)),
            pl.BlockSpec((1, length, GROUP_HEADS), lambda g: (g, 0, 0)),
            pl.BlockSpec((1, length, GROUP_HEADS), lambda g: (g, 0, 0)),
            pl.BlockSpec((1, GROUP_HEADS, length), lambda g: (g, 0, 0)),
            pl.BlockSpec((blocks, 1, GROUP_WIDTH), lambda g: (0, 0, g)),
            pl.BlockSpec((chunks, STATE, width), lambda g: (g, 0, 0)),
            pl.BlockSpec((1, GROUP_WIDTH), group_column),
            pl.BlockSpec((1, GROUP_WIDTH), group_column),
        ],
        out_specs=pl.BlockSpec((length, GROUP_WIDTH), group_column),
        out_shape=jax.ShapeDtypeStruct((length, INNER), jnp.bfloat16),
        scratch_shapes=[
            pltpu.VMEM((STATE, GROUP_WIDTH), jnp.float32),
            pltpu.VMEM((BLOCK, GROUP_WIDTH), jnp.bfloat16),
        ],
        compiler_params=pltpu.CompilerParams(vmem_limit_bytes=VMEM_LIMIT),
        name="mix",
    )(active, active, active, decay, gap, gap_rows, ending, entering, skip, gain)


def per_device(
    tokens,
    in_weight,
    step_weight,
    step_bias,
    decay_rate,
    skip_gain,
    filter_taps,
    filter_bias,
    norm_gain,
):
    token_rows = tokens[0]
    length = token_rows.shape[0]
    blocks = length // BLOCK
    parts = lax.axis_size("ctx")
    weight = lax.all_gather(in_weight, "dp")
    rim = lax.ppermute(token_rows[length - RIM :], "ctx", [(s, s + 1) for s in range(parts - 1)])
    rows = jnp.concatenate([rim, token_rows], axis=0)

    step_raw = jnp.dot(token_rows, step_weight, preferred_element_type=jnp.float32).astype(
        jnp.bfloat16
    )
    step_size = jax.nn.softplus(step_raw.astype(jnp.float32) + step_bias)
    decay = jnp.cumsum((-step_size * decay_rate).reshape(blocks, BLOCK, HEADS), axis=1) * LOG2E
    ending = decay[:, -1, :]
    decay = decay.reshape(length, HEADS)
    gap = decay - jnp.log2(step_size)
    grouped = lambda array: array.reshape(length, GROUPS, GROUP_HEADS).transpose(1, 0, 2)
    decay_columns, gap_columns = grouped(decay), grouped(gap)
    gap_rows = gap.T.reshape(GROUPS, GROUP_HEADS, length)
    ending_lanes = jnp.repeat(ending, HEAD_DIM, axis=1)[:, None, :]
    totals = lax.all_gather(jnp.sum(ending, axis=0), "ctx")
    mine = lax.axis_index("ctx")
    heads_each = HEADS // parts
    totals = lax.dynamic_slice_in_dim(totals, mine * heads_each, heads_each, 1)
    factors = jnp.repeat(jnp.exp2(totals), HEAD_DIM, axis=1)[:, None, :]

    active = project(rows, weight, filter_taps, filter_bias[None], 256)
    states = device_states(active, gap_columns, ending_lanes, parts)
    owned = lax.all_to_all(states, "ctx", split_axis=0, concat_axis=0, tiled=True)
    running = jnp.zeros(owned.shape[1:], jnp.float32)
    entering = []
    for source in range(parts):
        entering.append(running.astype(jnp.bfloat16))
        running = running * factors[source] + owned[source].astype(jnp.float32)
    entering = lax.all_to_all(jnp.stack(entering), "ctx", split_axis=0, concat_axis=0, tiled=True)
    skip = jnp.repeat(skip_gain, HEAD_DIM)[None]
    return mix(
        active, decay_columns, gap_columns, gap_rows, ending_lanes, entering, skip, norm_gain[None]
    )[None]


def solution(mesh):
    in_specs = (P("dp", "ctx", None), P(None, "dp"), P(), P(), P(), P(), P(), P(), P())
    out_specs = P("dp", "ctx", None)
    return jax.shard_map(
        per_device, mesh=mesh, in_specs=in_specs, out_specs=out_specs, check_vma=False
    )
```

time: 563 us -> 278 us (0.49); the launches traced: 554 us -> 277 us
  waiting for transfers between devices: 234 us -> 146 us
  local copies, waits for them, and re-layouts: 85 us -> 9.14 us
  matrix products: 69.2 us -> 0.84 us
  blocking collectives: 97.4 us -> 31.6 us
  Pallas kernels: 0 us -> 51.9 us
  other arithmetic: 28.3 us -> 8.24 us
  starting transfers between devices: 26.1 us -> 15.5 us
    all_to_all x1 -> x0, blocking collectives: 97.4 us -> none  [head_layout(): lax.all_to_all(mixed_rows, 'ctx', split_axis=0, concat_axis=1, tiled=True)]
    all_to_all x4 -> x2, waiting for transfers between devices: 106 us -> 21.1 us  [the longest x1 21.1 us: per_device(): lax.all_to_all(jnp.stack(entering), 'ctx', split_axis=0, concat_axis=0, t...]
    dot_general x9 -> x0, matrix products: 66.9 us -> none  [the longest x1 15.9 us: ssd_group(): jnp.einsum('khpn,ktn->kthp', entering, output_rows.astype(jnp.float32), p...]
    pallas_call x0 -> x3, Pallas kernels: none -> 51.9 us  [the longest x1 26.6 us: project(): pl.pallas_call(project_kernel, grid=(shards, tiles), in_specs=[pl.BlockSp...]
    convert_element_type x6 -> x0, local copies, waits for them, and re-layouts: 41.3 us -> none  [the longest x2 17.6 us: ssd_group(): value_rows.astype(jnp.float32)]
    unnamed x0 -> x1, blocking collectives: none -> 31.6 us
    convert_element_type x6 -> x0, other arithmetic: 17.4 us -> none  [the longest x1 6.71 us: sequence_filter(): jax.nn.silu(filter_rows(rim_rows, projected, filter_taps, filter_bias))]
    all_to_all x4 -> x2, starting transfers between devices: 22.7 us -> 10.5 us  [the longest x1 5.52 us: per_device(): lax.all_to_all(states, 'ctx', split_axis=0, concat_axis=0, tiled=True)]
  transfers between devices with their start and end apart: 6 -> 4, of which waited for: 5 -> 2; matrix products, arithmetic and copies ran while one was open for 12% -> 4% of each run, Pallas kernels for 0% -> 0%
where the time goes in v1:
time: 278 us; the launch traced here: 277 us
  waiting for transfers between devices  146 us (53%)
  Pallas kernels  51.9 us (19%)
  blocking collectives  31.6 us (11%)
  starting transfers between devices  15.5 us (6%)
  between operations  14.2 us (5%)
  local copies, waits for them, and re-layouts  9.14 us (3%)
  other arithmetic  8.24 us (3%)
    all_gather x1, waiting for transfers between devices, per_device(): weight = lax.all_gather(in_weight, 'dp')  124 us
    unnamed x1, blocking collectives  31.6 us
    pallas_call x1, Pallas kernels, project(): pl.pallas_call(project_kernel, grid=(shards, tiles), in_specs=[pl.BlockSp...  26.6 us
    all_to_all x1, waiting for transfers between devices, per_device(): lax.all_to_all(jnp.stack(entering), 'ctx', split_axis=0, concat_axis=0, t...  21.1 us
    pallas_call x1, Pallas kernels, mix(): pl.pallas_call(mix_kernel, grid=(GROUPS,), in_specs=[pl.BlockSpec((length...  17.1 us
    pallas_call x1, Pallas kernels, device_states(): pl.pallas_call(states_kernel, grid=(GROUPS,), in_specs=[pl.BlockSpec((len...  8.18 us
  transfers between devices with their start and end apart: 4, of which 2 were waited for; matrix products, arithmetic and copies ran while one was open for 4% of the time, Pallas kernels for 0%

profile of v1, /device:TPU:0, one launch (start us, length us, event | category | flops | bytes accessed | tf_op | source)
XLA Modules:
  0.0 277.0 jit_solution(6488351738034058187)
XLA Ops:
  6.6 0.7 all-gather.4.cloned.1.call-update
  7.3 0.9 copy-done.1
  8.2 4.9 %collective-permute-start = (bf16[16,2048]{1,0:T(8,128)(2,1)S(1)}, bf16[16,2048]{1,0:T(8,128)(2,1)S(1)}, u32[]{:S(2)}, u32[]{:S(2)}) collective-permute-start(bf16[16,2048]{1,0:T(8,128)(2,1)S(1)} %slice_bitcast_fusion), channel_id=1, source_target_pairs={{0,1},{1,2},{2,3},{3,4},{4,5},{5,6},{6,7},{8,9},{9,10},{10,11},{11... | collective-permute-start | bytes 196616 | tf_op jit(solution)/shard_map/ppermute | solution.py:242
  13.1 0.8 negate_multiply_fusion
  14.0 1.2 reduce-window.6
  15.2 0.2 slice_reduce_fusion
  15.4 0.1 bitcast_bitcast_fusion
  15.6 1.3 copy.24
  16.9 0.2 slice_reduce_fusion.1
  17.1 0.1 broadcast_in_dim.48
  17.2 0.7 broadcast_in_dim_reshape.7.ending_ref
  17.9 1.5 pad_maximum_fusion.rows_ref
  19.4 123.9 %all-gather.4.cloned.1.call-done = bf16[8192,1280]{1,0:T(8,128)(2,1)} async-done(((bf16[2048,1280]{1,0:T(8,128)(2,1)}), bf16[8192,1280]{1,0:T(8,128)(2,1)}) %all-gather.4.cloned.1.call-update) | async-done | bytes 20971536 | tf_op jit(solution)/shard_map/all_gather | solution.py:241
  143.3 26.6 %project.1.values_ref.input_ref.output_ref = bf16[512,5120]{1,0:T(8,128)(2,1)} custom-call(bf16[528,2048]{1,0:T(8,128)(2,1)} %pad_maximum_fusion.rows_ref, bf16[4,2048,1280]{2,1,0:T(8,128)(2,1)} %bitcast.56, f32[4,5120]{1,0:T(4,128)} %taps_ref.1, f32[1,5120]{1,0:T(1,128)} %bitcast.65), custom_call_target="tpu_custom_call" | custom-call | tf_op jit(solution)/shard_map/project/pallas_call | solution.py:42
  169.9 8.2 %states.1 = bf16[8,128,512]{2,1,0:T(8,128)(2,1)} custom-call(bf16[512,5120]{1,0:T(8,128)(2,1)} %project.1.values_ref.input_ref.output_ref, bf16[512,5120]{1,0:T(8,128)(2,1)} %project.1.values_ref.input_ref.output_ref, f32[4,512,16]{2,1,0:T(8,128)} %bitcast.57, f32[2,1,4096]{2,1,0:T(1,128)} %broadcast_in_dim_reshape.7.ending_ref), custom_call_target="tpu_custom_call" | custom-call | tf_op jit(solution)/shard_map/states/pallas_call | solution.py:98
  178.1 5.5 %all-to-all-start = ((bf16[8,128,512]{2,1,0:T(8,128)(2,1)}), bf16[8,128,512]{2,1,0:T(8,128)(2,1)S(1)}, u32[]{:S(2)}, u32[]{:S(2)}) async-start(bf16[8,128,512]{2,1,0:T(8,128)(2,1)} %states.1), calls=%async_computation | async-start | bytes 2097152 | tf_op jit(solution)/shard_map/all_to_all | solution.py:265
  183.6 0.6 dynamic-slice
  184.8 0.2 dynamic-update-slice
  185.1 0.1 reshape.234
  185.2 31.6 %all-reduce.1 = f32[8,64]{1,0:T(8,128)S(1)} all-reduce(f32[8,64]{1,0:T(8,128)S(1)} %reshape.234), channel_id=3, replica_groups=mesh['dp'=4,'ctx'=8] {'ctx'}, use_global_device_ids=true, to_apply=%add | all-reduce | flops 512 | bytes 4096
  216.8 0.1 multiply_exponential_fusion
  216.9 0.1 broadcast_in_dim.50
  216.9 0.1 mul_broadcast_in_dim.13
  217.0 0.1 broadcast_in_dim.51
  217.1 0.1 broadcast_in_dim.52
  217.2 0.1 broadcast_in_dim.53
  217.2 0.1 broadcast_in_dim.54
  217.4 0.1 broadcast_in_dim.56
  217.5 0.1 broadcast_in_dim.58
  217.7 0.1 broadcast_in_dim.60
  217.8 0.1 broadcast_in_dim.62
  217.9 0.7 broadcast_dynamic-update-slice_fusion
  218.6 0.7 fusion.9
  219.3 0.7 fusion.8
  220.0 0.7 convert_dynamic-update-slice_fusion.1
  220.7 0.8 fusion.7
  221.5 0.8 convert_dynamic-update-slice_fusion
  222.2 0.7 fusion.6
  222.9 0.7 fusion.10
  223.7 5.0 %all-to-all-start.1 = ((bf16[8,128,512]{2,1,0:T(8,128)(2,1)}), bf16[8,128,512]{2,1,0:T(8,128)(2,1)S(1)}, u32[]{:S(2)}, u32[]{:S(2)}) async-start(bf16[8,128,512]{2,1,0:T(8,128)(2,1)} %fusion.10), calls=%async_computation.1 | async-start | bytes 2097152 | tf_op jit(solution)/shard_map/all_to_all | solution.py:271
  228.7 0.1 copy.21
  228.8 0.1 reshape_reshape.3
  228.9 1.3 copy.22
  230.2 0.1 broadcast_in_dim.63
  230.3 0.7 broadcast_in_dim_reshape.8.skip_ref
  231.0 21.1 %all-to-all-done.1.entering_ref = bf16[8,128,512]{2,1,0:T(8,128)(2,1)S(1)} async-done(((bf16[8,128,512]{2,1,0:T(8,128)(2,1)}), bf16[8,128,512]{2,1,0:T(8,128)(2,1)S(1)}, u32[]{:S(2)}, u32[]{:S(2)}) %all-to-all-start.1) | async-done | bytes 1048608 | tf_op jit(solution)/shard_map/all_to_all | solution.py:271
  252.1 1.0 copy-done.2
  253.1 17.1 %mix.1 = bf16[512,4096]{1,0:T(8,128)(2,1)} custom-call(bf16[512,5120]{1,0:T(8,128)(2,1)} %project.1.values_ref.input_ref.output_ref, bf16[512,5120]{1,0:T(8,128)(2,1)} %project.1.values_ref.input_ref.output_ref, bf16[512,5120]{1,0:T(8,128)(2,1)} %project.1.values_ref.input_ref.output_ref, f32[4,512,16]{2,1,0:T(8,128)} %bitcast.60, f32[4,512,16]{2,1,0:T(8,128)} %bitcast.58, ...), custom_call_target="tpu_custom_call" | custom-call | tf_op jit(solution)/shard_map/mix/pallas_call | solution.py:200
  (29 shorter events, 0.4 us)
Async XLA Ops:
  6.5 6.5 %copy-start = (bf16[2048,64]{0,1:T(8,128)(2,1)S(1)}, bf16[2048,64]{0,1:T(8,128)(2,1)}, u32[]{:S(2)}) copy-start(bf16[2048,64]{0,1:T(8,128)(2,1)} %param.11) | copy-start | bytes 786436
  6.5 1.6 copy-start.1
  6.5 6.5 %copy-start.4 = (f32[64]{0:T(128)S(1)}, f32[64]{0:T(128)}, u32[]{:S(2)}) copy-start(f32[64]{0:T(128)} %param.13) | copy-start | bytes 772
  6.5 6.6 %copy-start.5 = (f32[64]{0:T(128)S(1)}, f32[64]{0:T(128)}, u32[]{:S(2)}) copy-start(f32[64]{0:T(128)} %param.12) | copy-start | bytes 772
  6.5 136.7 %all-gather.4.cloned.1.call-start = ((), (), s32[]{:S(2)}) async-start(), calls=%async_computation.2 | async-start | bytes 26214400 | tf_op jit(solution)/shard_map/all_gather | solution.py:241
  8.2 9.7 %collective-permute-start = (bf16[16,2048]{1,0:T(8,128)(2,1)S(1)}, bf16[16,2048]{1,0:T(8,128)(2,1)S(1)}, u32[]{:S(2)}, u32[]{:S(2)}) collective-permute-start(bf16[16,2048]{1,0:T(8,128)(2,1)S(1)} %slice_bitcast_fusion), channel_id=1, source_target_pairs={{0,1},{1,2},{2,3},{3,4},{4,5},{5,6},{6,7},{8,9},{9,10},{10,11},{11... | collective-permute-start | bytes 196616 | tf_op jit(solution)/shard_map/ppermute | solution.py:242
  15.6 3.8 %copy-start.3 = (f32[512,64]{0,1:T(8,128)}, f32[512,64]{0,1:T(8,128)S(1)}, u32[]{:S(2)}) copy-start(f32[512,64]{0,1:T(8,128)S(1)} %multiply_subtract_fusion) | copy-start | bytes 393220
  169.9 13.7 %copy-start.7 = (u32[32]{0:T(128)S(1)}, u32[32]{0:T(128)}, u32[]{:S(2)}) copy-start(u32[32]{0:T(128)} %constant.28) | copy-start | bytes 388
  178.1 40.5 %all-to-all-start = ((bf16[8,128,512]{2,1,0:T(8,128)(2,1)}), bf16[8,128,512]{2,1,0:T(8,128)(2,1)S(1)}, u32[]{:S(2)}, u32[]{:S(2)}) async-start(bf16[8,128,512]{2,1,0:T(8,128)(2,1)} %states.1), calls=%async_computation | async-start | bytes 2097152 | tf_op jit(solution)/shard_map/all_to_all | solution.py:265
  222.9 7.3 %copy-start.6 = (f32[64]{0:T(128)S(1)}, f32[64]{0:T(128)}, u32[]{:S(2)}) copy-start(f32[64]{0:T(128)} %param.14) | copy-start | bytes 772
  223.7 28.4 %all-to-all-start.1 = ((bf16[8,128,512]{2,1,0:T(8,128)(2,1)}), bf16[8,128,512]{2,1,0:T(8,128)(2,1)S(1)}, u32[]{:S(2)}, u32[]{:S(2)}) async-start(bf16[8,128,512]{2,1,0:T(8,128)(2,1)} %fusion.10), calls=%async_computation.1 | async-start | bytes 2097152 | tf_op jit(solution)/shard_map/all_to_all | solution.py:271
  252.0 1.0 copy-start.2
Sparse Core Ops, SparseCore 0:
  8.9 134.2 all-gather.3

commit v2 on v1

--- a/solution.py
+++ b/solution.py
@@ -21,37 +21,234 @@
 VMEM_LIMIT = 60 * 2**20
 
 
-def project_kernel(rows_ref, weight_ref, taps_ref, bias_ref, active_ref):
+CHUNKS = 4
+SENT_ORDER = (2, 3, 0, 1)
+TILE = 256
+
+
+def flipped(index, bit):
+    return index + bit - 2 * bit * ((index // bit) % 2)
+
+
+def gather_project_kernel(
+    rows_ref,
+    weight_ref,
+    taps_ref,
+    bias_ref,
+    active_ref,
+    held,
+    sums,
+    local_sem,
+    own_send,
+    own_recv,
+    x_send,
+    x_recv,
+    y_send,
+    y_recv,
+    z_send,
+    z_recv,
+    core_send,
+    core_recv,
+):
+    me_dp, me_ctx = lax.axis_index("dp"), lax.axis_index("ctx")
+    depth, width = weight_ref.shape
     length = active_ref.shape[0]
-    projected = jnp.dot(rows_ref[...], weight_ref[0], preferred_element_type=jnp.float32)
-    projected = projected.astype(jnp.bfloat16).astype(jnp.float32)
-    taps = taps_ref[...]
-    count = taps.shape[0]
-    summed = bias_ref[...] + taps[count - 1 : count] * projected[RIM:]
-    for k in range(count - 1):
-        first = RIM - (count - 1) + k
-        summed = summed + taps[k : k + 1] * projected[first : first + length]
-    active_ref[...] = (summed / (1.0 + jnp.exp(-summed))).astype(jnp.bfloat16)
-
-
-def project(rows, weight, taps, bias, tile):
+    quarter = depth // 4
+    piece = quarter // CHUNKS
+    partner, across, beyond = flipped(me_dp, 1), flipped(me_dp, 2), flipped(flipped(me_dp, 1), 2)
+    core_peer, x_peer = (partner, me_ctx), (across, me_ctx)
+    y_peer, z_peer = (me_dp, flipped(me_ctx, 1)), (me_dp, flipped(me_ctx, 2))
+    mine = me_ctx % 4
+    quarters = (mine, flipped(mine, 1), flipped(mine, 2), 3 - mine)
+
+    barrier = pltpu.get_barrier_semaphore()
+    for peer in (core_peer, x_peer, y_peer, z_peer):
+        pl.semaphore_signal(
+            barrier, inc=1, device_id=peer, device_id_type=pl.DeviceIdType.MESH
+        )
+    pl.semaphore_wait(barrier, 4)
+
+    def span(kind, chunk):
+        start = quarters[kind] * quarter + chunk * piece
+        return pl.ds(pl.multiple_of(start, piece), piece)
+
+    def remote(source, target, send, recv, peer):
+        return pltpu.make_async_remote_copy(
+            src_ref=source,
+            dst_ref=target,
+            send_sem=send,
+            recv_sem=recv,
+            device_id=peer,
+            device_id_type=pl.DeviceIdType.MESH,
+        )
+
+    started = []
+
+    def start(copy):
+        copy.start()
+        started.append(copy)
+
+    local = pltpu.make_async_copy(weight_ref, held.at[me_dp], local_sem)
+    local.start()
+    start(remote(weight_ref, held.at[me_dp], own_send, own_recv, core_peer))
+    x_slots = [(0, chunk) for chunk in SENT_ORDER] + [(3, 0), (3, 1)]
+    for slot, (kind, chunk) in enumerate(x_slots):
+        rows = span(kind, chunk)
+        start(
+            remote(
+                weight_ref.at[rows, :],
+                held.at[me_dp, rows, :],
+                x_send.at[slot],
+                x_recv.at[slot],
+                x_peer,
+            )
+        )
+
+    def landed(kind, chunk, recv, send, peer):
+        part = held.at[across, span(kind, chunk), :]
+        remote(part, part, send, recv, peer).wait_recv()
+
+    def forward(kind, chunk, send, recv, peer):
+        part = held.at[across, span(kind, chunk), :]
+        start(remote(part, part, send, recv, peer))
+
+    def to_core(kind, chunk):
+        slot = kind * CHUNKS + chunk
+        forward(kind, chunk, core_send.at[slot], core_recv.at[slot], core_peer)
+
+    def from_x(slot):
+        kind, chunk = x_slots[slot]
+        landed(kind, chunk, x_recv.at[slot], x_send.at[slot], x_peer)
+        if slot < CHUNKS:
+            forward(kind, chunk, y_send.at[slot], y_recv.at[slot], y_peer)
+            forward(kind, chunk, z_send.at[slot], z_recv.at[slot], z_peer)
+        to_core(kind, chunk)
+
+    def from_y(slot):
+        kind, chunk = (1, SENT_ORDER[slot]) if slot < CHUNKS else (3, 3)
+        landed(kind, chunk, y_recv.at[slot], y_send.at[slot], y_peer)
+        if (kind, chunk) == (1, 2):
+            forward(kind, chunk, z_send.at[CHUNKS], z_recv.at[CHUNKS], z_peer)
+        to_core(kind, chunk)
+
+    def from_z(slot):
+        kind, chunk = (2, SENT_ORDER[slot]) if slot < CHUNKS else (3, 2)
+        landed(kind, chunk, z_recv.at[slot], z_send.at[slot], z_peer)
+        if (kind, chunk) == (2, 3):
+            forward(kind, chunk, y_send.at[CHUNKS], y_recv.at[CHUNKS], y_peer)
+        to_core(kind, chunk)
+
+    def from_core(kind):
+        for chunk in range(CHUNKS):
+            part = held.at[beyond, span(kind, chunk), :]
+            slot = kind * CHUNKS + chunk
+            remote(part, part, core_send.at[slot], core_recv.at[slot], core_peer).wait_recv()
+
+    def finish(total, shard, tile):
+        lanes = pl.ds(pl.multiple_of(shard * width + tile * TILE, 128), TILE)
+        projected = total.astype(jnp.bfloat16).astype(jnp.float32)
+        taps = taps_ref[:, lanes]
+        count = taps.shape[0]
+        summed = bias_ref[:, lanes] + taps[count - 1 : count] * projected[RIM:]
+        for k in range(count - 1):
+            first = RIM - (count - 1) + k
+            summed = summed + taps[k : k + 1] * projected[first : first + length]
+        active_ref[:, lanes] = (summed / (1.0 + jnp.exp(-summed))).astype(jnp.bfloat16)
+
+    def whole_shard(shard):
+        @pl.loop(0, width // TILE)
+        def _(tile):
+            lanes = pl.ds(pl.multiple_of(tile * TILE, TILE), TILE)
+            finish(
+                jnp.dot(
+                    rows_ref[...], held[shard, :, lanes], preferred_element_type=jnp.float32
+                ),
+                shard,
+                tile,
+            )
+
+    def part_shard(shard, at, kinds, first, last):
+        @pl.loop(0, width // TILE)
+        def _(tile):
+            lanes = pl.ds(pl.multiple_of(tile * TILE, TILE), TILE)
+            total = None if first else sums[at, :, lanes]
+            for kind in kinds:
+                deep = pl.ds(pl.multiple_of(quarters[kind] * quarter, quarter), quarter)
+                product = jnp.dot(
+                    rows_ref[:, deep],
+                    held[shard, deep, lanes],
+                    preferred_element_type=jnp.float32,
+                )
+                total = product if total is None else total + product
+            if last:
+                finish(total, shard, tile)
+            else:
+                sums[at, :, lanes] = total
+
+    local.wait()
+    whole_shard(me_dp)
+    from_x(0)
+    remote(weight_ref, held.at[partner], own_send, own_recv, core_peer).wait_recv()
+    whole_shard(partner)
+    from_x(1)
+    from_y(0)
+    from_z(0)
+    from_x(2)
+    from_z(1)
+    from_y(1)
+    from_x(3)
+    part_shard(across, 0, (0,), True, False)
+    from_core(0)
+    part_shard(beyond, 1, (0,), True, False)
+    from_y(2)
+    from_z(2)
+    from_y(3)
+    from_z(3)
+    part_shard(across, 0, (1, 2), False, False)
+    from_core(1)
+    from_core(2)
+    part_shard(beyond, 1, (1, 2), False, False)
+    from_x(4)
+    from_x(5)
+    from_y(4)
+    from_z(4)
+    part_shard(across, 0, (3,), False, True)
+    from_core(3)
+    part_shard(beyond, 1, (3,), False, True)
+    for copy in started:
+        copy.wait_send()
+
+
+def gather_project(rows, weight, taps, bias):
     length = rows.shape[0] - RIM
-    shards, depth, width = weight.shape
-    tiles = width // tile
-    column = lambda s, j: (0, s * tiles + j)
+    depth, width = weight.shape
+    shards = lax.axis_size("dp")
+    dma = pltpu.SemaphoreType.DMA
+    vmem = pl.BlockSpec(memory_space=pltpu.VMEM)
     return pl.pallas_call(
-        project_kernel,
-        grid=(shards, tiles),
-        in_specs=[
-            pl.BlockSpec(rows.shape, lambda s, j: (0, 0)),
-            pl.BlockSpec((1, depth, tile), lambda s, j: (s, 0, j)),
-            pl.BlockSpec((taps.shape[0], tile), column),
-            pl.BlockSpec((1, tile), column),
+        gather_project_kernel,
+        in_specs=[vmem, pl.BlockSpec(memory_space=pl.ANY), vmem, vmem],
+        out_specs=vmem,
+        out_shape=jax.ShapeDtypeStruct((length, shards * width), jnp.bfloat16),
+        scratch_shapes=[
+            pltpu.VMEM((shards, depth, width), jnp.bfloat16),
+            pltpu.VMEM((2, length + RIM, width), jnp.float32),
+            dma,
+            dma,
+            dma,
+            dma((CHUNKS + 2,)),
+            dma((CHUNKS + 2,)),
+            dma((CHUNKS + 1,)),
+            dma((CHUNKS + 1,)),
+            dma((CHUNKS + 1,)),
+            dma((CHUNKS + 1,)),
+            dma((4 * CHUNKS,)),
+            dma((4 * CHUNKS,)),
         ],
-        out_specs=pl.BlockSpec((length, tile), column),
-        out_shape=jax.ShapeDtypeStruct((length, shards * width), jnp.bfloat16),
-        compiler_params=pltpu.CompilerParams(vmem_limit_bytes=VMEM_LIMIT),
-        name="project",
+        compiler_params=pltpu.CompilerParams(
+            vmem_limit_bytes=VMEM_LIMIT, collective_id=0, has_side_effects=True
+        ),
+        name="gather_project",
     )(rows, weight, taps, bias)
 
 
@@ -238,7 +435,6 @@
     length = token_rows.shape[0]
     blocks = length // BLOCK
     parts = lax.axis_size("ctx")
-    weight = lax.all_gather(in_weight, "dp")
     rim = lax.ppermute(token_rows[length - RIM :], "ctx", [(s, s + 1) for s in range(parts - 1)])
     rows = jnp.concatenate([rim, token_rows], axis=0)
 
@@ -260,7 +456,7 @@
     totals = lax.dynamic_slice_in_dim(totals, mine * heads_each, heads_each, 1)
     factors = jnp.repeat(jnp.exp2(totals), HEAD_DIM, axis=1)[:, None, :]
 
-    active = project(rows, weight, filter_taps, filter_bias[None], 256)
+    active = gather_project(rows, in_weight, filter_taps, filter_bias[None])
     states = device_states(active, gap_columns, ending_lanes, parts)
     owned = lax.all_to_all(states, "ctx", split_axis=0, concat_axis=0, tiled=True)
     running = jnp.zeros(owned.shape[1:], jnp.float32)

time: 278 us -> 176 us (0.63)
  waiting for transfers between devices: 146 us -> 21 us
  Pallas kernels: 51.9 us -> 87.4 us
  between operations: 14.2 us -> 0.8 us
    all_gather x1 -> x0, waiting for transfers between devices: 124 us -> none  [per_device(): weight = lax.all_gather(in_weight, 'dp')]
    pallas_call x1, Pallas kernels: 26.6 us -> 62.1 us  [gather_project(): pl.pallas_call(gather_project_kernel, in_specs=[vmem, pl.BlockSpec(memory...]
  transfers between devices with their start and end apart: 4 -> 3, of which waited for: 2 -> 1; matrix products, arithmetic and copies ran while one was open for 4% -> 7% of each run, Pallas kernels for 0% -> 0%
where the time goes in v2:
time: 176 us; the launch traced here: 175 us
  Pallas kernels  87.4 us (50%)
  blocking collectives  30.6 us (17%)
  waiting for transfers between devices  21 us (12%)
  starting transfers between devices  15.7 us (9%)
  local copies, waits for them, and re-layouts  9.18 us (5%)
  other arithmetic  8.25 us (5%)
  matrix products  2.44 us (1%)
    pallas_call x1, Pallas kernels, gather_project(): pl.pallas_call(gather_project_kernel, in_specs=[vmem, pl.BlockSpec(memory...  62.1 us
    unnamed x1, blocking collectives  30.6 us
    all_to_all x1, waiting for transfers between devices, per_device(): lax.all_to_all(jnp.stack(entering), 'ctx', split_axis=0, concat_axis=0, t...  21 us
    pallas_call x1, Pallas kernels, mix(): pl.pallas_call(mix_kernel, grid=(GROUPS,), in_specs=[pl.BlockSpec((length...  17.1 us
    pallas_call x1, Pallas kernels, device_states(): pl.pallas_call(states_kernel, grid=(GROUPS,), in_specs=[pl.BlockSpec((len...  8.22 us
    all_to_all x1, starting transfers between devices, per_device(): lax.all_to_all(jnp.stack(entering), 'ctx', split_axis=0, concat_axis=0, t...  5.63 us
    all_to_all x1, starting transfers between devices, per_device(): lax.all_to_all(states, 'ctx', split_axis=0, concat_axis=0, tiled=True)  5.2 us
    ppermute x1, starting transfers between devices, per_device(): lax.ppermute(token_rows[length - RIM:], 'ctx', [(s, s + 1) for s in range...  4.89 us
  transfers between devices with their start and end apart: 3, of which 1 were waited for; matrix products, arithmetic and copies ran while one was open for 7% of the time, Pallas kernels for 0%

profile of v2, /device:TPU:0, one launch (start us, length us, event | category | flops | bytes accessed | tf_op | source)
XLA Modules:
  0.0 175.4 jit_solution(9773154509662527699)
XLA Ops:
  0.0 0.9 slice_bitcast_fusion
  0.9 4.9 %collective-permute-start = (bf16[16,2048]{1,0:T(8,128)(2,1)S(1)}, bf16[16,2048]{1,0:T(8,128)(2,1)S(1)}, u32[]{:S(2)}, u32[]{:S(2)}) collective-permute-start(bf16[16,2048]{1,0:T(8,128)(2,1)S(1)} %slice_bitcast_fusion), channel_id=1, source_target_pairs={{0,1},{1,2},{2,3},{3,4},{4,5},{5,6},{6,7},{8,9},{9,10},{10,11},{11... | collective-permute-start | bytes 196616 | tf_op jit(solution)/shard_map/ppermute | solution.py:438
  5.8 2.4 %negate_multiply_fusion = (f32[512,64]{0,1:T(8,128)S(1)}, f32[512,64]{0,1:T(8,128)S(1)}) fusion(f32[64]{0:T(128)} %param.13, f32[64]{0:T(128)} %param.12, bf16[2048,64]{0,1:T(8,128)(2,1)S(1)} %copy-done, bf16[1,512,2048]{2,1,0:T(8,128)(2,1)} %param.9), kind=kOutput, calls=%fused_computation.30 | convolution fusion | flops 134578176 | bytes 2621952 | tf_op jit(solution)/shard_map/dot_general | solution.py:441
  8.3 1.2 reduce-window.6
  9.5 0.2 slice_reduce_fusion
  9.7 0.1 bitcast_bitcast_fusion
  9.9 0.2 slice_reduce_fusion.1
  10.1 0.1 broadcast_in_dim.48
  10.2 0.7 broadcast_in_dim_reshape.7.ending_ref
  10.9 1.4 copy.24
  12.3 1.5 pad_maximum_fusion.rows_ref
  13.8 62.1 %gather_project.1.values_ref.input_ref.output_ref = bf16[512,5120]{1,0:T(8,128)(2,1)} custom-call(bf16[528,2048]{1,0:T(8,128)(2,1)} %pad_maximum_fusion.rows_ref, bf16[2048,1280]{1,0:T(8,128)(2,1)} %weight_ref.1, f32[4,5120]{1,0:T(4,128)} %taps_ref.1, f32[1,5120]{1,0:T(1,128)} %bitcast.63), custom_call_target="tpu_custom_call" | custom-call | tf_op jit(solution)/shard_map/gather_project/pallas_call | solution.py:228
  75.9 8.2 %states.1 = bf16[8,128,512]{2,1,0:T(8,128)(2,1)} custom-call(bf16[512,5120]{1,0:T(8,128)(2,1)} %gather_project.1.values_ref.input_ref.output_ref, bf16[512,5120]{1,0:T(8,128)(2,1)} %gather_project.1.values_ref.input_ref.output_ref, f32[4,512,16]{2,1,0:T(8,128)} %bitcast.55, f32[2,1,4096]{2,1,0:T(1,128)} %broadcast_in_dim_reshape.7.ending_ref), custom_call_target="tpu_custom_call" | custom-call | tf_op jit(solution)/shard_map/states/pallas_call | solution.py:295
  84.1 5.2 %all-to-all-start = ((bf16[8,128,512]{2,1,0:T(8,128)(2,1)}), bf16[8,128,512]{2,1,0:T(8,128)(2,1)S(1)}, u32[]{:S(2)}, u32[]{:S(2)}) async-start(bf16[8,128,512]{2,1,0:T(8,128)(2,1)} %states.1), calls=%async_computation | async-start | bytes 2097152 | tf_op jit(solution)/shard_map/all_to_all | solution.py:461
  89.3 0.6 dynamic-slice
  90.5 0.2 dynamic-update-slice
  90.8 0.1 reshape.233
  90.9 30.6 %all-reduce.1 = f32[8,64]{1,0:T(8,128)S(1)} all-reduce(f32[8,64]{1,0:T(8,128)S(1)} %reshape.233), channel_id=2, replica_groups=mesh['dp'=4,'ctx'=8] {'ctx'}, use_global_device_ids=true, to_apply=%add | all-reduce | flops 512 | bytes 4096
  121.5 0.1 multiply_exponential_fusion
  121.6 0.1 broadcast_in_dim.61
  121.7 0.1 broadcast_in_dim.62
  121.7 0.1 broadcast_in_dim.59
  121.8 0.1 broadcast_in_dim.60
  121.9 0.1 broadcast_in_dim.57
  122.0 0.1 broadcast_in_dim.58
  122.0 0.1 broadcast_in_dim.55
  122.1 0.1 broadcast_in_dim.56
  122.2 0.1 broadcast_in_dim.53
  122.3 0.1 broadcast_in_dim.54
  122.4 0.1 broadcast_in_dim.52
  122.6 0.1 mul_broadcast_in_dim.13
  122.6 0.7 broadcast_dynamic-update-slice_fusion
  123.3 0.7 fusion.9
  124.0 0.7 fusion.8
  124.7 0.7 convert_dynamic-update-slice_fusion.1
  125.4 0.8 fusion.7
  126.2 0.8 convert_dynamic-update-slice_fusion
  127.0 0.7 fusion.6
  127.7 0.7 fusion.10
  128.4 5.6 %all-to-all-start.1 = ((bf16[8,128,512]{2,1,0:T(8,128)(2,1)}), bf16[8,128,512]{2,1,0:T(8,128)(2,1)S(1)}, u32[]{:S(2)}, u32[]{:S(2)}) async-start(bf16[8,128,512]{2,1,0:T(8,128)(2,1)} %fusion.10), calls=%async_computation.1 | async-start | bytes 2097152 | tf_op jit(solution)/shard_map/all_to_all | solution.py:467
  134.0 0.1 copy.21
  134.1 0.1 broadcast_in_dim.63
  134.2 0.7 broadcast_in_dim_reshape.8.skip_ref
  134.9 0.1 reshape_reshape.3
  135.0 1.3 copy.22
  136.4 21.0 %all-to-all-done.1.entering_ref = bf16[8,128,512]{2,1,0:T(8,128)(2,1)S(1)} async-done(((bf16[8,128,512]{2,1,0:T(8,128)(2,1)}), bf16[8,128,512]{2,1,0:T(8,128)(2,1)S(1)}, u32[]{:S(2)}, u32[]{:S(2)}) %all-to-all-start.1) | async-done | bytes 1048608 | tf_op jit(solution)/shard_map/all_to_all | solution.py:467
  157.3 1.0 copy-done.2
  158.3 17.1 %mix.1 = bf16[512,4096]{1,0:T(8,128)(2,1)} custom-call(bf16[512,5120]{1,0:T(8,128)(2,1)} %gather_project.1.values_ref.input_ref.output_ref, bf16[512,5120]{1,0:T(8,128)(2,1)} %gather_project.1.values_ref.input_ref.output_ref, bf16[512,5120]{1,0:T(8,128)(2,1)} %gather_project.1.values_ref.input_ref.output_ref, f32[4,512,16]{2,1,0:T(8,128)} %bitcast.58, ...), custom_call_target="tpu_custom_call" | custom-call | tf_op jit(solution)/shard_map/mix/pallas_call | solution.py:397
  (22 shorter events, 0.3 us)
Async XLA Ops:
  0.0 5.8 %copy-start = (bf16[2048,64]{0,1:T(8,128)(2,1)S(1)}, bf16[2048,64]{0,1:T(8,128)(2,1)}, u32[]{:S(2)}) copy-start(bf16[2048,64]{0,1:T(8,128)(2,1)} %param.11) | copy-start | bytes 786436
  0.9 11.4 %collective-permute-start = (bf16[16,2048]{1,0:T(8,128)(2,1)S(1)}, bf16[16,2048]{1,0:T(8,128)(2,1)S(1)}, u32[]{:S(2)}, u32[]{:S(2)}) collective-permute-start(bf16[16,2048]{1,0:T(8,128)(2,1)S(1)} %slice_bitcast_fusion), channel_id=1, source_target_pairs={{0,1},{1,2},{2,3},{3,4},{4,5},{5,6},{6,7},{8,9},{9,10},{10,11},{11... | collective-permute-start | bytes 196616 | tf_op jit(solution)/shard_map/ppermute | solution.py:438
  8.2 4.0 %copy-start.1 = (bf16[1,512,2048]{2,1,0:T(8,128)(2,1)S(1)}, bf16[1,512,2048]{2,1,0:T(8,128)(2,1)}, u32[]{:S(2)}) copy-start(bf16[1,512,2048]{2,1,0:T(8,128)(2,1)} %param.9) | copy-start | bytes 6291460
  9.9 3.9 %copy-start.3 = (f32[512,64]{0,1:T(8,128)}, f32[512,64]{0,1:T(8,128)S(1)}, u32[]{:S(2)}) copy-start(f32[512,64]{0,1:T(8,128)S(1)} %multiply_subtract_fusion) | copy-start | bytes 393220
  75.9 13.4 %copy-start.5 = (u32[32]{0:T(128)S(1)}, u32[32]{0:T(128)}, u32[]{:S(2)}) copy-start(u32[32]{0:T(128)} %constant.28) | copy-start | bytes 388
  84.1 39.2 %all-to-all-start = ((bf16[8,128,512]{2,1,0:T(8,128)(2,1)}), bf16[8,128,512]{2,1,0:T(8,128)(2,1)S(1)}, u32[]{:S(2)}, u32[]{:S(2)}) async-start(bf16[8,128,512]{2,1,0:T(8,128)(2,1)} %states.1), calls=%async_computation | async-start | bytes 2097152 | tf_op jit(solution)/shard_map/all_to_all | solution.py:461
  126.2 8.0 %copy-start.4 = (f32[64]{0:T(128)S(1)}, f32[64]{0:T(128)}, u32[]{:S(2)}) copy-start(f32[64]{0:T(128)} %param.14) | copy-start | bytes 772
  128.4 28.9 %all-to-all-start.1 = ((bf16[8,128,512]{2,1,0:T(8,128)(2,1)}), bf16[8,128,512]{2,1,0:T(8,128)(2,1)S(1)}, u32[]{:S(2)}, u32[]{:S(2)}) async-start(bf16[8,128,512]{2,1,0:T(8,128)(2,1)} %fusion.10), calls=%async_computation.1 | async-start | bytes 2097152 | tf_op jit(solution)/shard_map/all_to_all | solution.py:467
  157.3 1.0 copy-start.2

commit v3 on v2

--- a/solution.py
+++ b/solution.py
@@ -17,6 +17,7 @@
 GROUP_WIDTH = GROUP_HEADS * HEAD_DIM
 INNER = HEADS * HEAD_DIM
 RIM = 16
+EXCHANGED = 16
 LOG2E = math.log2(math.e)
 VMEM_LIMIT = 60 * 2**20
 
@@ -420,6 +421,154 @@
     )(active, active, active, decay, gap, gap_rows, ending, entering, skip, gain)
 
 
+def exchange_kernel(
+    state_ref,
+    factor_ref,
+    entering_ref,
+    other_state,
+    other_factor,
+    arriving,
+    leaving,
+    answer,
+    factor_send,
+    factor_recv,
+    state_send,
+    state_recv,
+    chain_send,
+    chain_recv,
+    answer_send,
+    answer_recv,
+):
+    me_dp, me = lax.axis_index("dp"), lax.axis_index("ctx")
+    count = lax.axis_size("ctx")
+    half = other_state.shape[0]
+    parity = me % 2
+    first, other_first = parity * half, (1 - parity) * half
+    partner = (me_dp, flipped(me, 1))
+    after, before = (me_dp, (me + 2) % count), (me_dp, (me + count - 2) % count)
+
+    barrier = pltpu.get_barrier_semaphore()
+    for peer in (partner, after, before):
+        pl.semaphore_signal(
+            barrier, inc=1, device_id=peer, device_id_type=pl.DeviceIdType.MESH
+        )
+    pl.semaphore_wait(barrier, 3)
+
+    def remote(source, target, send, recv, peer):
+        return pltpu.make_async_remote_copy(
+            src_ref=source,
+            dst_ref=target,
+            send_sem=send,
+            recv_sem=recv,
+            device_id=peer,
+            device_id_type=pl.DeviceIdType.MESH,
+        )
+
+    factors = remote(
+        factor_ref.at[pl.ds(other_first, half)], other_factor, factor_send, factor_recv, partner
+    )
+    factors.start()
+    shared, chained, answers = [], [], []
+    for i in range(half):
+        shared.append(
+            remote(
+                state_ref.at[other_first + i],
+                other_state.at[i],
+                state_send.at[i],
+                state_recv.at[i],
+                partner,
+            )
+        )
+        shared[i].start()
+        chained.append(
+            remote(leaving.at[i], arriving.at[i], chain_send.at[i], chain_recv.at[i], after)
+        )
+        answers.append(
+            remote(
+                answer.at[i],
+                entering_ref.at[first + i],
+                answer_send.at[i],
+                answer_recv.at[i],
+                partner,
+            )
+        )
+
+    @pl.when(me < 2)
+    def _():
+        arriving[...] = jnp.zeros_like(arriving)
+
+    factors.wait_recv()
+    even = parity == 0
+    for i in range(half):
+        shared[i].wait_recv()
+
+        @pl.when(me >= 2)
+        def _():
+            chained[i].wait_recv()
+
+        own, theirs = state_ref[first + i].astype(jnp.float32), other_state[i].astype(jnp.float32)
+        own_factor, their_factor = factor_ref[first + i], other_factor[i]
+        early, late = jnp.where(even, own, theirs), jnp.where(even, theirs, own)
+        early_factor = jnp.where(even, own_factor, their_factor)
+        late_factor = jnp.where(even, their_factor, own_factor)
+        start = arriving[i].astype(jnp.float32)
+        middle = start * early_factor + early
+        leaving[i] = (middle * late_factor + late).astype(jnp.bfloat16)
+
+        @pl.when(me < count - 2)
+        def _():
+            chained[i].start()
+
+        answer[i] = jnp.where(even, middle, start).astype(jnp.bfloat16)
+        answers[i].start()
+        entering_ref[first + i] = jnp.where(even, start, middle).astype(jnp.bfloat16)
+
+    for i in range(half):
+        remote(
+            answer.at[i],
+            entering_ref.at[other_first + i],
+            answer_send.at[i],
+            answer_recv.at[i],
+            partner,
+        ).wait_recv()
+        shared[i].wait_send()
+        answers[i].wait_send()
+
+        @pl.when(me < count - 2)
+        def _():
+            chained[i].wait_send()
+
+    factors.wait_send()
+
+
+def exchange(states, factors):
+    parts = states.shape[0]
+    half = parts // 2
+    dma = pltpu.SemaphoreType.DMA
+    vmem = pl.BlockSpec(memory_space=pltpu.VMEM)
+    piece = (half,) + states.shape[1:]
+    return pl.pallas_call(
+        exchange_kernel,
+        in_specs=[vmem, vmem],
+        out_specs=vmem,
+        out_shape=jax.ShapeDtypeStruct(states.shape, jnp.bfloat16),
+        scratch_shapes=[
+            pltpu.VMEM(piece, jnp.bfloat16),
+            pltpu.VMEM((half,) + factors.shape[1:], jnp.float32),
+            pltpu.VMEM(piece, jnp.bfloat16),
+            pltpu.VMEM(piece, jnp.bfloat16),
+            pltpu.VMEM(piece, jnp.bfloat16),
+            dma,
+            dma,
+        ]
+        + [dma((half,))] * 6,
+        compiler_params=pltpu.CompilerParams(
+            vmem_limit_bytes=VMEM_LIMIT, collective_id=1, has_side_effects=True
+        ),
+        name="exchange",
+    )(states, factors)
+
+
 def per_device(
     tokens,
     in_weight,
@@ -450,21 +599,13 @@
     decay_columns, gap_columns = grouped(decay), grouped(gap)
     gap_rows = gap.T.reshape(GROUPS, GROUP_HEADS, length)
     ending_lanes = jnp.repeat(ending, HEAD_DIM, axis=1)[:, None, :]
-    totals = lax.all_gather(jnp.sum(ending, axis=0), "ctx")
-    mine = lax.axis_index("ctx")
-    heads_each = HEADS // parts
-    totals = lax.dynamic_slice_in_dim(totals, mine * heads_each, heads_each, 1)
-    factors = jnp.repeat(jnp.exp2(totals), HEAD_DIM, axis=1)[:, None, :]
+    parts_width = INNER // EXCHANGED
+    factors = jnp.repeat(jnp.exp2(jnp.sum(ending, axis=0)), HEAD_DIM)
+    factors = factors.reshape(EXCHANGED, 1, parts_width)
 
     active = gather_project(rows, in_weight, filter_taps, filter_bias[None])
-    states = device_states(active, gap_columns, ending_lanes, parts)
-    owned = lax.all_to_all(states, "ctx", split_axis=0, concat_axis=0, tiled=True)
-    running = jnp.zeros(owned.shape[1:], jnp.float32)
-    entering = []
-    for source in range(parts):
-        entering.append(running.astype(jnp.bfloat16))
-        running = running * factors[source] + owned[source].astype(jnp.float32)
-    entering = lax.all_to_all(jnp.stack(entering), "ctx", split_axis=0, concat_axis=0, tiled=True)
+    states = device_states(active, gap_columns, ending_lanes, EXCHANGED)
+    entering = exchange(states, factors)
     skip = jnp.repeat(skip_gain, HEAD_DIM)[None]
     return mix(
         active, decay_columns, gap_columns, gap_rows, ending_lanes, entering, skip, norm_gain[None]

time: 176 us -> 135 us (0.77)
  blocking collectives: 30.6 us -> 0 us
  Pallas kernels: 87.4 us -> 118 us
  waiting for transfers between devices: 21 us -> 0.01 us
  starting transfers between devices: 15.7 us -> 5.02 us
  other arithmetic: 8.25 us -> 3.08 us
  local copies, waits for them, and re-layouts: 9.18 us -> 6.44 us
    unnamed x1 -> x0, blocking collectives: 30.6 us -> none
    pallas_call x0 -> x1, Pallas kernels: none -> 30.3 us  [exchange(): pl.pallas_call(exchange_kernel, in_specs=[vmem, vmem], out_specs=vmem, ou...]
    all_to_all x2 -> x0, waiting for transfers between devices: 21 us -> none  [the longest x1 21 us: per_device(): lax.all_to_all(jnp.stack(entering), 'ctx', split_axis=0, concat_axis=0, t...]
    all_to_all x2 -> x0, starting transfers between devices: 10.8 us -> none  [the longest x1 5.63 us: per_device(): lax.all_to_all(jnp.stack(entering), 'ctx', split_axis=0, concat_axis=0, t...]
    unnamed x7 -> x1, other arithmetic: 4.47 us -> 0.11 us
    unnamed x16 -> x8, local copies, waits for them, and re-layouts: 2.5 us -> 0.02 us
  transfers between devices with their start and end apart: 3 -> 1, of which waited for: 1 -> 0; matrix products, arithmetic and copies ran while one was open for 7% -> 7% of each run, Pallas kernels for 0% -> 0%
where the time goes in v3:
time: 135 us
  Pallas kernels  118 us (87%)
  local copies, waits for them, and re-layouts  6.44 us (5%)
  starting transfers between devices  5.02 us (4%)
  other arithmetic  3.08 us (2%)
  matrix products  2.44 us (2%)
    pallas_call x1, Pallas kernels, gather_project(): pl.pallas_call(gather_project_kernel, in_specs=[vmem, pl.BlockSpec(memory...  62.1 us
    pallas_call x1, Pallas kernels, exchange(): pl.pallas_call(exchange_kernel, in_specs=[vmem, vmem], out_specs=vmem, ou...  30.3 us
    pallas_call x1, Pallas kernels, mix(): pl.pallas_call(mix_kernel, grid=(GROUPS,), in_specs=[pl.BlockSpec((length...  17.1 us
    pallas_call x1, Pallas kernels, device_states(): pl.pallas_call(states_kernel, grid=(GROUPS,), in_specs=[pl.BlockSpec((len...  8.2 us
    ppermute x1, starting transfers between devices, per_device(): lax.ppermute(token_rows[length - RIM:], 'ctx', [(s, s + 1) for s in range...  5.02 us
  transfers between devices with their start and end apart: 1, of which 0 were waited for; matrix products, arithmetic and copies ran while one was open for 7% of the time, Pallas kernels for 0%

profile of v3, /device:TPU:0, one launch (start us, length us, event | category | flops | bytes accessed | tf_op | source)
XLA Modules:
  0.0 134.8 jit_solution(16420911952574938799)
XLA Ops:
  0.0 0.0 copy-start
  0.0 0.9 slice_bitcast_fusion
  0.9 0.0 copy-start.3
  0.9 5.0 %collective-permute-start = (bf16[16,2048]{1,0:T(8,128)(2,1)S(1)}, bf16[16,2048]{1,0:T(8,128)(2,1)S(1)}, u32[]{:S(2)}, u32[]{:S(2)}) collective-permute-start(bf16[16,2048]{1,0:T(8,128)(2,1)S(1)} %slice_bitcast_fusion), channel_id=1, source_target_pairs={{0,1},{1,2},{2,3},{3,4},{4,5},{5,6},{6,7},{8,9},{9,10},{10,11},{11... | collective-permute-start | bytes 196616 | tf_op jit(solution)/shard_map/ppermute | solution.py:587
  5.9 0.0 copy-done
  5.9 2.4 %negate_multiply_fusion = (f32[512,64]{0,1:T(8,128)S(1)}, f32[512,64]{0,1:T(8,128)S(1)}) fusion(f32[64]{0:T(128)} %param.13, f32[64]{0:T(128)} %param.12, bf16[2048,64]{0,1:T(8,128)(2,1)S(1)} %copy-done, bf16[1,512,2048]{2,1,0:T(8,128)(2,1)} %param.9), kind=kOutput, calls=%fused_computation.12 | convolution fusion | flops 134578176 | bytes 2621952 | tf_op jit(solution)/shard_map/dot_general | solution.py:590
  8.4 1.2 reduce-window.6
  9.6 0.2 slice_reduce_fusion
  9.8 0.0 copy-start.1
  9.8 0.1 bitcast_bitcast_fusion
  10.0 0.2 slice_reduce_fusion.1
  10.2 0.0 copy-start.2
  10.3 0.1 copy.21
  10.4 0.0 copy-done.3
  10.4 0.1 broadcast_in_dim.26
  10.4 0.7 broadcast_in_dim_reshape.7.skip_ref
  11.1 0.1 reshape_reshape.4
  11.2 0.1 exp2.18
  11.3 0.1 broadcast_in_dim.24
  11.4 0.7 broadcast_in_dim.25.factor_ref
  12.1 0.1 broadcast_in_dim.23
  12.2 0.7 broadcast_in_dim_reshape.6.ending_ref
  12.9 1.4 %copy.22 = f32[512,4,16]{2,0,1:T(8,128)} copy(f32[512,4,16]{0,2,1:T(8,128)S(1)} %reshape_reshape.4) | data formatting | bytes 262144 | tf_op jit(solution)/shard_map/reshape;reshape | solution.py:598
  14.3 1.3 copy.24
  15.6 0.0 collective-permute-done
  15.6 0.0 copy-done.1
  15.6 1.5 %pad_maximum_fusion.rows_ref = bf16[528,2048]{1,0:T(8,128)(2,1)} fusion(bf16[512,2048]{1,0:T(8,128)(2,1)S(1)} %bitcast.42, bf16[16,2048]{1,0:T(8,128)(2,1)S(1)} %collective-permute-done), kind=kLoop, calls=%fused_computation | loop fusion | flops 4325376 | bytes 4325376 | tf_op jit(solution)/shard_map/concatenate | solution.py:588
  17.1 0.0 copy-done.2
  17.1 62.1 %gather_project.1.values_ref.input_ref.output_ref = bf16[512,5120]{1,0:T(8,128)(2,1)} custom-call(bf16[528,2048]{1,0:T(8,128)(2,1)} %pad_maximum_fusion.rows_ref, bf16[2048,1280]{1,0:T(8,128)(2,1)} %weight_ref.1, f32[4,5120]{1,0:T(4,128)} %taps_ref.1, f32[1,5120]{1,0:T(1,128)} %bitcast.48), custom_call_target="tpu_custom_call" | custom-call | tf_op jit(solution)/shard_map/gather_project/pallas_call | solution.py:229
  79.2 8.2 %states.1.state_ref = bf16[16,128,256]{2,1,0:T(8,128)(2,1)} custom-call(bf16[512,5120]{1,0:T(8,128)(2,1)} %gather_project.1.values_ref.input_ref.output_ref, bf16[512,5120]{1,0:T(8,128)(2,1)} %gather_project.1.values_ref.input_ref.output_ref, f32[4,512,16]{2,1,0:T(8,128)} %bitcast.40, f32[2,1,4096]{2,1,0:T(1,128)} %broadcast_in_dim_reshape.6.ending_ref), custom_call_target="tpu_custom_call" | custom-call | tf_op jit(solution)/shard_map/states/pallas_call | solution.py:296
  87.4 30.3 %exchange.1.entering_ref = bf16[16,128,256]{2,1,0:T(8,128)(2,1)} custom-call(bf16[16,128,256]{2,1,0:T(8,128)(2,1)} %states.1.state_ref, f32[16,1,256]{2,1,0:T(1,128)} %broadcast_in_dim.25.factor_ref), custom_call_target="tpu_custom_call" | custom-call | tf_op jit(solution)/shard_map/exchange/pallas_call | solution.py:550
  117.7 17.1 %mix.1 = bf16[512,4096]{1,0:T(8,128)(2,1)} custom-call(bf16[512,5120]{1,0:T(8,128)(2,1)} %gather_project.1.values_ref.input_ref.output_ref, bf16[512,5120]{1,0:T(8,128)(2,1)} %gather_project.1.values_ref.input_ref.output_ref, bf16[512,5120]{1,0:T(8,128)(2,1)} %gather_project.1.values_ref.input_ref.output_ref, f32[4,512,16]{2,1,0:T(8,128)} %bitcast.43, ...), custom_call_target="tpu_custom_call" | custom-call | tf_op jit(solution)/shard_map/mix/pallas_call | solution.py:398
  (6 shorter events, 0.1 us)
Async XLA Ops:
  0.0 5.9 %copy-start = (bf16[2048,64]{0,1:T(8,128)(2,1)S(1)}, bf16[2048,64]{0,1:T(8,128)(2,1)}, u32[]{:S(2)}) copy-start(bf16[2048,64]{0,1:T(8,128)(2,1)} %param.11) | copy-start | bytes 786436
  0.9 9.5 %copy-start.3 = (f32[64]{0:T(128)S(1)}, f32[64]{0:T(128)}, u32[]{:S(2)}) copy-start(f32[64]{0:T(128)} %param.14) | copy-start | bytes 772
  0.9 14.7 %collective-permute-start = (bf16[16,2048]{1,0:T(8,128)(2,1)S(1)}, bf16[16,2048]{1,0:T(8,128)(2,1)S(1)}, u32[]{:S(2)}, u32[]{:S(2)}) collective-permute-start(bf16[16,2048]{1,0:T(8,128)(2,1)S(1)} %slice_bitcast_fusion), channel_id=1, source_target_pairs={{0,1},{1,2},{2,3},{3,4},{4,5},{5,6},{6,7},{8,9},{9,10},{10,11},{11... | collective-permute-start | bytes 196616 | tf_op jit(solution)/shard_map/ppermute | solution.py:587
  9.8 5.8 %copy-start.1 = (bf16[1,512,2048]{2,1,0:T(8,128)(2,1)S(1)}, bf16[1,512,2048]{2,1,0:T(8,128)(2,1)}, u32[]{:S(2)}) copy-start(bf16[1,512,2048]{2,1,0:T(8,128)(2,1)} %param.9) | copy-start | bytes 6291460
  10.2 6.9 %copy-start.2 = (f32[512,64]{0,1:T(8,128)}, f32[512,64]{0,1:T(8,128)S(1)}, u32[]{:S(2)}) copy-start(f32[512,64]{0,1:T(8,128)S(1)} %multiply_subtract_fusion) | copy-start | bytes 393220
